TPU v7x, 32 devices: a whole 2x2x4 slice. The times are simulated.
32 devices in a mesh: ctx: 16 (over z, x, core), tp: 2 (over y).
Axes of the slice: x: 2, y: 2, z: 4, core: 2. Of those that a mesh axis runs over, the one named last changes fastest.
Arguments:
- token_ids: int32 [12288], P('ctx'), may hold values from 0 to 511
- embed_table: bfloat16 [512, 4096], replicated, may hold values from -6 to 6
- norm_gain: float32 [4096], replicated, may hold values from 0.25 to 1.75
- w_in: bfloat16 [4096, 3, 2048], P(None, None, 'tp'), may hold values from -0.09375 to 0.09375
- short_taps: float32 [3, 3, 2048], P(None, None, 'tp'), may hold values from -3 to 3
- long_filter: bfloat16 [2048, 12288], P('tp', 'ctx'), may hold values from -0.0546875 to 0.0546875
- skip_gain: float32 [2048], P('tp'), may hold values from 0.5 to 2
- w_out: bfloat16 [2048, 4096], P(None, 'tp'), may hold values from -0.125 to 0.125
Outputs:
- mixed: bfloat16 [12288, 4096], P('ctx', 'tp')
All inputs are finite; a program needn't handle non-finite values.
Results may differ from a plain program's by a relative error of at most 0.0095.
Values may be sent and summed in bfloat16 or wider, within the bound.
A program may use at most 192 MiB of HBM per device.

v0:
```python
import math
import jax
import jax.numpy as jnp
from jax import lax
from jax.sharding import PartitionSpec as P

norm_eps = 1e-06


def shifted(block, axis, distance):
    devices = range(lax.axis_size(axis))
    route = [(i - distance, i) for i in devices if i - distance in devices]
    return lax.ppermute(block, axis, route)


def angle_table(outer, inner, period):
    product = (
        jnp.arange(outer, dtype=jnp.int32)[:, None]
        * jnp.arange(inner, dtype=jnp.int32)[None, :]
        % period
    )
    phase = product.astype(jnp.float32) * (2.0 * math.pi / period)
    return (jnp.cos(phase), jnp.sin(phase))


def contract(form, left, right):
    return jnp.einsum(
        form, left, right, precision=lax.Precision.HIGHEST, preferred_element_type=jnp.float32
    )


def forward_transform(signal, tables):
    cos_rows, sin_rows, cos_twist, sin_twist, cos_cols, sin_cols = tables
    first_real = contract("kn,cnm->ckm", cos_rows, signal)
    first_imag = -contract("kn,cnm->ckm", sin_rows, signal)
    turned_real = first_real * cos_twist + first_imag * sin_twist
    turned_imag = first_imag * cos_twist - first_real * sin_twist
    spec_real = contract("ckm,mj->ckj", turned_real, cos_cols) + contract(
        "ckm,mj->ckj", turned_imag, sin_cols
    )
    spec_imag = contract("ckm,mj->ckj", turned_imag, cos_cols) - contract(
        "ckm,mj->ckj", turned_real, sin_cols
    )
    return (spec_real, spec_imag)


def inverse_transform(spec_real, spec_imag, tables, period):
    cos_rows, sin_rows, cos_twist, sin_twist, cos_cols, sin_cols = tables
    back_real = contract("ckj,mj->ckm", spec_real, cos_cols) - contract(
        "ckj,mj->ckm", spec_imag, sin_cols
    )
    back_imag = contract("ckj,mj->ckm", spec_imag, cos_cols) + contract(
        "ckj,mj->ckm", spec_real, sin_cols
    )
    untwist_real = back_real * cos_twist - back_imag * sin_twist
    untwist_imag = back_imag * cos_twist + back_real * sin_twist
    signal = contract("kn,ckm->cnm", cos_rows, untwist_real) - contract(
        "kn,ckm->cnm", sin_rows, untwist_imag
    )
    return signal / period


def causal_conv(signal, kernel):
    channels = signal.shape[0]
    length = signal.shape[1]
    col_count = min(256, length)
    row_count = 2 * length // col_count
    half_rows = length // col_count
    cos_rows, sin_rows = angle_table(row_count, half_rows, row_count)
    cos_twist, sin_twist = angle_table(row_count, col_count, row_count * col_count)
    cos_cols, sin_cols = angle_table(col_count, col_count, col_count)
    tables = (cos_rows, sin_rows, cos_twist, sin_twist, cos_cols, sin_cols)
    signal_real, signal_imag = forward_transform(
        signal.astype(jnp.float32).reshape(channels, half_rows, col_count), tables
    )
    kernel_real, kernel_imag = forward_transform(
        kernel.astype(jnp.float32).reshape(channels, half_rows, col_count), tables
    )
    joint_real = signal_real * kernel_real - signal_imag * kernel_imag
    joint_imag = signal_real * kernel_imag + signal_imag * kernel_real
    result = inverse_transform(joint_real, joint_imag, tables, row_count * col_count)
    return result.reshape(channels, length)


def local(token_ids, embed_table, norm_gain, w_in, short_taps, long_filter, skip_gain, w_out):
    vocab = embed_table.shape[0]
    one_hot = (token_ids[:, None] == jnp.arange(vocab, dtype=jnp.int32)[None, :]).astype(
        jnp.bfloat16
    )
    embedded = jnp.dot(one_hot, embed_table, preferred_element_type=jnp.float32)
    scale = lax.rsqrt(jnp.mean(embedded * embedded, axis=1, keepdims=True) + norm_eps)
    normed = (embedded * scale * norm_gain).astype(jnp.bfloat16)
    width = w_in.shape[0]
    chan_part = w_in.shape[2]
    flat_proj = jnp.dot(
        normed, w_in.reshape(width, 3 * chan_part), preferred_element_type=jnp.float32
    ).astype(jnp.bfloat16)
    projected = jnp.transpose(flat_proj.reshape(-1, 3, chan_part), (1, 2, 0))
    positions = projected.shape[2]
    edge = projected[:, :, positions - 2 :]
    prior = shifted(edge, "ctx", 1)
    extended = jnp.concatenate([prior, projected], axis=2).astype(jnp.float32)
    shortened = (
        short_taps[0][:, :, None] * extended[:, :, 2:]
        + short_taps[1][:, :, None] * extended[:, :, 1 : positions + 1]
        + short_taps[2][:, :, None] * extended[:, :, 0:positions]
    ).astype(jnp.bfloat16)
    query_side = shortened[0]
    key_side = shortened[1]
    value_side = shortened[2]
    local_channels = shortened.shape[1]
    groups = lax.axis_size("ctx")
    owned = local_channels // groups

    def spread(array):
        return array.reshape(groups, owned, array.shape[-1])

    first_channel = lax.axis_index("ctx") * owned
    own_skip = lax.dynamic_slice_in_dim(skip_gain, first_channel, owned)[:, None]
    product_local = (key_side.astype(jnp.float32) * value_side.astype(jnp.float32)).astype(
        jnp.bfloat16
    )
    arrived = (
        lax.all_to_all(spread(product_local), "ctx", split_axis=0, concat_axis=2, tiled=True),
        lax.all_to_all(spread(long_filter), "ctx", split_axis=0, concat_axis=2, tiled=True),
    )
    product = arrived[0].reshape(owned, -1)
    filter_full = arrived[1].reshape(owned, -1)
    convolved = causal_conv(product, filter_full)
    outgoing = (convolved + own_skip * product.astype(jnp.float32)).astype(jnp.bfloat16)
    returned = lax.all_to_all(
        outgoing.reshape(1, owned, -1), "ctx", split_axis=2, concat_axis=0, tiled=True
    )
    returned = returned.reshape(local_channels, positions)
    gated = (query_side.astype(jnp.float32) * returned.astype(jnp.float32)).astype(jnp.bfloat16)
    width_part = w_out.shape[1]
    projected_out = jnp.dot(
        lax.all_gather(gated, "tp", axis=0, tiled=True).T, w_out, preferred_element_type=jnp.float32
    )
    residual = lax.dynamic_slice_in_dim(embedded, lax.axis_index("tp") * width_part, width_part, 1)
    return (residual + projected_out).astype(jnp.bfloat16)


def solution(mesh):
    return jax.shard_map(
        local,
        mesh=mesh,
        in_specs=(
            P("ctx"),
            P(),
            P(),
            P(None, None, "tp"),
            P(None, None, "tp"),
            P("tp", "ctx"),
            P("tp"),
            P(None, "tp"),
        ),
        out_specs=P("ctx", "tp"),
        check_vma=False,
    )
```

profile of v0, /device:TPU:0, one launch (start us, length us, event | category | flops | bytes accessed | tf_op | source)
XLA Modules:
  0.0 508.5 jit_solution(8029366977371177981)
XLA Ops:
  6.5 7.4 %all-to-all-start.1 = ((bf16[16,64,768]{2,1,0:T(8,128)(2,1)}), bf16[16,64,768]{2,1,0:T(8,128)(2,1)S(1)}, u32[]{:S(2)}, u32[]{:S(2)}) async-start(bf16[16,64,768]{2,1,0:T(8,128)(2,1)} %bitcast.149), calls=%async_computation.1 | async-start | bytes 3145728 | tf_op jit(solution)/shard_map/all_to_all | solution.py:125
  13.9 8.8 %multiply_reduce_fusion = (f32[768]{0:T(1024)S(1)}, f32[768,4096]{1,0:T(8,128)}) fusion(bf16[512,4096]{1,0:T(8,128)(2,1)} %param.9, s32[768]{0:T(1024)} %param.8), kind=kOutput, calls=%fused_computation.1 | convolution fusion | flops 3227909376 | bytes 16783360 | tf_op jit(solution)/shard_map/dot_general | solution.py:90
  22.7 33.5 %copy.32 = bf16[4096,3,1024]{0,2,1:T(8,128)(2,1)} copy(bf16[4096,3,1024]{2,0,1:T(8,128)(2,1)} %param.11) | data formatting | bytes 50331648 | tf_op args[3]
  56.2 27.9 %fusion.24 = bf16[768,3072]{1,0:T(8,128)(2,1)} fusion(bf16[4096,3072]{0,1:T(8,128)(2,1)} %bitcast.138, f32[768,4096]{1,0:T(8,128)} %get-tuple-element.11, f32[4096]{0:T(1024)S(1)} %copy-done.9, f32[768]{0:T(1024)S(1)} %add_rsqrt_fusion), kind=kOutput, calls=%fused_computation.39 | convolution fusion | flops 19339149312 | bytes 42486784 | tf_op jit(solution)/shard_map/dot_general | solution.py:95
  84.1 6.6 %copy.33 = bf16[768,3072]{0,1:T(8,128)(2,1)} copy(bf16[768,3072]{1,0:T(8,128)(2,1)} %fusion.24) | data formatting | bytes 9437184 | tf_op jit(solution)/shard_map/convert_element_type | solution.py:97
  90.7 1.4 slice.40
  92.2 0.3 copy.34
  92.5 2.6 collective-permute-start
  95.1 0.4 fusion.86
  95.5 0.8 dynamic_slice.7
  96.3 0.0 collective-permute-done
  96.3 0.4 copy.35
  96.7 4.8 maximum_convert_fusion
  101.5 8.1 %fusion.1 = bf16[3,1024,768]{2,1,0:T(8,128)(2,1)S(1)} fusion(f32[3,1024,770]{2,1,0:T(8,128)S(1)} %maximum_convert_fusion, f32[3,1024]{1,0:T(4,128)S(1)} %get-tuple-element.8, f32[3,1024]{1,0:T(4,128)S(1)} %get-tuple-element.9, f32[3,1024]{1,0:T(4,128)S(1)} %get-tuple-element.7), kind=kLoop, calls=%fused_computation.4 | loop fusion | flops 14155776 | bytes 33067008 | tf_op jit(solution)/shard_map/convert_element_type | solution.py:107
  109.7 2.2 copy-done.3
  111.9 1.5 multiply_convert_fusion.4
  113.4 0.0 all-to-all-done.1
  113.4 1.1 copy-done.7
  114.6 7.2 %all-to-all-start = ((bf16[16,64,768]{2,1,0:T(8,128)(2,1)}), bf16[16,64,768]{2,1,0:T(8,128)(2,1)S(1)}, u32[]{:S(2)}, u32[]{:S(2)}) async-start(bf16[16,64,768]{2,1,0:T(8,128)(2,1)} %bitcast.147), calls=%async_computation | async-start | bytes 3145728 | tf_op jit(solution)/shard_map/all_to_all | solution.py:124
  121.7 0.6 all-gather.2.cloned.1.call-start
  122.3 3.5 copy.37
  125.8 3.7 reshape.134
  129.5 4.3 fusion.92
  133.9 2.8 fusion.97
  136.6 9.2 %fusion.10 = f32[64,96,256]{2,1,0:T(8,128)} fusion(f32[96,64,256]{2,0,1:T(8,128)S(1)} %fusion.97, f32[96,64,256]{2,0,1:T(8,128)S(1)} %fusion.92, f32[96,256]{1,0:T(8,128)S(1)} %get-tuple-element.12, f32[96,256]{1,0:T(8,128)S(1)} %get-tuple-element.13), kind=kOutput, calls=%fused_computation.15 | convolution fusion | flops 4839047168 | bytes 19070976 | tf_op jit(solution)/shard_map/ckm,mj->ckj/dot_general | solution.py:27
  145.9 9.3 %fusion.6 = f32[64,96,256]{2,1,0:T(8,128)} fusion(f32[96,64,256]{2,0,1:T(8,128)S(1)} %fusion.97, f32[96,64,256]{2,0,1:T(8,128)S(1)} %fusion.92, f32[96,256]{1,0:T(8,128)S(1)} %get-tuple-element.12, f32[96,256]{1,0:T(8,128)S(1)} %get-tuple-element.13), kind=kOutput, calls=%fused_computation.11 | convolution fusion | flops 4839047168 | bytes 19070976 | tf_op jit(solution)/shard_map/ckm,mj->ckj/dot_general | solution.py:27
  155.2 9.1 %fusion.8 = f32[64,96,256]{2,1,0:T(8,128)} fusion(f32[96,64,256]{2,0,1:T(8,128)S(1)} %fusion.97, f32[96,64,256]{2,0,1:T(8,128)S(1)} %fusion.92, f32[96,256]{1,0:T(8,128)S(1)} %get-tuple-element.12, f32[96,256]{1,0:T(8,128)S(1)} %get-tuple-element.13), kind=kOutput, calls=%fused_computation.13 | convolution fusion | flops 4839047168 | bytes 19070976 | tf_op jit(solution)/shard_map/ckm,mj->ckj/dot_general | solution.py:27
  164.4 0.0 all-to-all-done
  164.4 2.0 copy.36
  166.4 3.9 reshape.132
  170.3 4.4 fusion.94
  174.7 2.7 fusion.99
  177.5 9.2 %fusion.37 = f32[64,96,256]{2,1,0:T(8,128)} fusion(f32[64,256,96]{1,2,0:T(8,128)S(1)} %fusion.99, f32[64,256,96]{1,2,0:T(8,128)S(1)} %fusion.94, f32[96,256]{1,0:T(8,128)S(1)} %get-tuple-element.12, f32[96,256]{1,0:T(8,128)S(1)} %get-tuple-element.13), kind=kOutput, calls=%fused_computation.59 | convolution fusion | flops 4839047168 | bytes 19070976 | tf_op jit(solution)/shard_map/ckm,mj->ckj/dot_general | solution.py:27
  186.7 9.6 %fusion.41 = f32[64,96,256]{2,1,0:T(8,128)} fusion(f32[64,256,96]{1,2,0:T(8,128)S(1)} %fusion.99, f32[64,256,96]{1,2,0:T(8,128)S(1)} %fusion.94, f32[96,256]{1,0:T(8,128)S(1)} %get-tuple-element.12, f32[96,256]{1,0:T(8,128)S(1)} %get-tuple-element.13), kind=kOutput, calls=%fused_computation.61 | convolution fusion | flops 4839047168 | bytes 19070976 | tf_op jit(solution)/shard_map/ckm,mj->ckj/dot_general | solution.py:27
  196.2 9.3 %fusion.39 = f32[64,96,256]{2,1,0:T(8,128)} fusion(f32[64,256,96]{1,2,0:T(8,128)S(1)} %fusion.99, f32[64,256,96]{1,2,0:T(8,128)S(1)} %fusion.94, f32[96,256]{1,0:T(8,128)S(1)} %get-tuple-element.12, f32[96,256]{1,0:T(8,128)S(1)} %get-tuple-element.13), kind=kOutput, calls=%fused_computation.60 | convolution fusion | flops 4839047168 | bytes 19070976 | tf_op jit(solution)/shard_map/ckm,mj->ckj/dot_general | solution.py:27
  205.5 9.2 %fusion.35 = f32[64,96,256]{2,1,0:T(8,128)} fusion(f32[64,256,96]{1,2,0:T(8,128)S(1)} %fusion.99, f32[64,256,96]{1,2,0:T(8,128)S(1)} %fusion.94, f32[96,256]{1,0:T(8,128)S(1)} %get-tuple-element.12, f32[96,256]{1,0:T(8,128)S(1)} %get-tuple-element.13), kind=kOutput, calls=%fused_computation.58 | convolution fusion | flops 4839047168 | bytes 19070976 | tf_op jit(solution)/shard_map/ckm,mj->ckj/dot_general | solution.py:27
  214.7 24.4 %multiply_subtract_fusion = (f32[64,96,256]{2,1,0:T(8,128)}, f32[64,96,256]{2,1,0:T(8,128)}) fusion(f32[64,96,256]{2,1,0:T(8,128)} %fusion.8, f32[64,96,256]{2,1,0:T(8,128)} %fusion.35, f32[64,96,256]{2,1,0:T(8,128)} %fusion.39, f32[64,96,256]{2,1,0:T(8,128)} %fusion.10, f32[64,96,256]{2,1,0:T(8,128)} %fusion.6, f32[64,96,256]{2,1,0:T(8,128)} %fusion.41, ...), kind=kOutput, calls=%fused_computation.33 | convolution fusion | flops 4854775808 | bytes 69402624 | tf_op jit(solution)/shard_map/ckm,mj->ckj/dot_general | solution.py:27
  239.0 0.0 slice-start.2
  239.0 9.8 %fusion.51 = f32[64,96,256]{2,1,0:T(8,128)S(1)} fusion(f32[64,96,256]{2,1,0:T(8,128)} %get-tuple-element.6), kind=kOutput, calls=%fused_computation.71 | convolution fusion | flops 4832755712 | bytes 12582912 | tf_op jit(solution)/shard_map/ckj,mj->ckm/dot_general | solution.py:27
  248.9 0.0 slice-start.3
  248.9 6.3 %fusion.57 = f32[64,96,256]{2,1,0:T(8,128)S(1)} fusion(f32[64,96,256]{2,1,0:T(8,128)S(1)} %copy-done.2), kind=kOutput, calls=%fused_computation.77 | convolution fusion | flops 4832755712 | bytes 12582912 | tf_op jit(solution)/shard_map/ckj,mj->ckm/dot_general | solution.py:27
  255.2 6.7 %fusion.49 = f32[64,96,256]{2,1,0:T(8,128)S(1)} fusion(f32[64,96,256]{2,1,0:T(8,128)S(1)} %bitcast.137), kind=kOutput, calls=%fused_computation.69 | convolution fusion | flops 4832755712 | bytes 12582912 | tf_op jit(solution)/shard_map/ckj,mj->ckm/dot_general | solution.py:27
  261.9 8.9 %fusion.59 = f32[64,96,256]{2,1,0:T(8,128)} fusion(f32[64,96,256]{2,1,0:T(8,128)S(1)} %bitcast.137), kind=kOutput, calls=%fused_computation.79 | convolution fusion | flops 4832755712 | bytes 12582912 | tf_op jit(solution)/shard_map/ckj,mj->ckm/dot_general | solution.py:27
  270.8 8.3 %fusion.14 = f32[64,256,48]{1,2,0:T(8,128)} fusion(f32[96,256]{1,0:T(8,128)S(1)} %get-tuple-element.12, f32[96,256]{1,0:T(8,128)S(1)} %get-tuple-element.13, f32[64,96,256]{2,1,0:T(8,128)S(1)} %fusion.57, f32[64,96,256]{2,1,0:T(8,128)S(1)} %fusion.49, f32[64,96,256]{2,1,0:T(8,128)} %fusion.59, f32[64,96,256]{2,1,0:T(8,128)S(1)} %fusion.51), kind=kOutput, calls=%fused_computation.24 | convolution fusion | flops 913875456 | bytes 28508160 | tf_op jit(solution)/shard_map/kn,ckm->cnm/dot_general | solution.py:27
  279.1 8.9 %multiply_bitcast_fusion = f32[64,48,256]{2,1,0:T(8,128)} fusion(f32[64,256,48]{1,2,0:T(8,128)} %fusion.14, f32[96,256]{1,0:T(8,128)S(1)} %get-tuple-element.12, f32[96,256]{1,0:T(8,128)S(1)} %get-tuple-element.13, f32[64,96,256]{2,1,0:T(8,128)S(1)} %fusion.57, f32[64,96,256]{2,1,0:T(8,128)S(1)} %fusion.49, f32[64,96,256]{2,1,0:T(8,128)} %fusion.59, ...), kind=kOutput, calls=%fused_computation.45 | convolution fusion | flops 915448320 | bytes 31653888 | tf_op jit(solution)/shard_map/kn,ckm->cnm/dot_general | solution.py:27
  288.0 4.3 reshape.135
  292.3 0.3 convert_bitcast_fusion
  292.6 0.3 copy.42
  292.9 1.2 copy-done.6
  294.2 0.3 add_convert_fusion.1
  294.5 10.0 %copy.39 = bf16[1,64,12288]{1,0,2:T(2,128)(2,1)} copy(bf16[1,64,12288]{2,1,0:T(8,128)(2,1)S(1)} %add_convert_fusion.1) | data formatting | bytes 3145728 | tf_op jit(solution)/shard_map/convert_element_type | solution.py:130
  304.5 0.5 broadcast.134
  305.0 67.2 %reduce = bf16[12288,64]{1,0:T(8,128)(2,1)S(1)} reduce(bf16[12288,1,64]{2,1,0:T(2,128)(2,1)} %bitcast.139, bf16[]{:T(256)} %broadcast.134), dimensions={1}, to_apply=%bitcast.115.reduce_sub_computation | reduce | bytes 3145730
  372.1 3.2 reshape.144
  375.4 42.1 %all_to_all.39 = bf16[16,2,24576]{2,1,0:T(2,128)(2,1)S(1)} all-to-all(bf16[16,2,24576]{2,1,0:T(2,128)(2,1)} %reshape.144), channel_id=1, replica_groups=mesh['ctx'=16,'tp'=2] {'ctx'}, dimensions={0} | all-to-all | bytes 3145728 | tf_op jit(solution)/shard_map/all_to_all | solution.py:131
  417.5 7.8 %reshape.145 = bf16[12288,1,64]{2,1,0:T(2,128)(2,1)} reshape(bf16[16,2,24576]{2,1,0:T(2,128)(2,1)S(1)} %all_to_all.39) | data formatting | bytes 3145728
  425.3 11.9 %copy.40 = bf16[1,64,12288]{2,1,0:T(8,128)(2,1)S(1)} copy(bf16[1,64,12288]{1,0,2:T(2,128)(2,1)} %bitcast.140) | data formatting | bytes 3145728 | tf_op jit(solution)/shard_map/all_to_all | solution.py:131
  437.2 0.4 copy.43
  437.7 0.2 bitcast_bitcast_fusion
  437.9 1.8 copy.41
  439.7 3.2 fusion.25
  443.0 0.0 all-gather.2.cloned.1.call-update
  443.0 45.5 %all-gather.2.cloned.1.call-done = bf16[2048,768]{1,0:T(8,128)(2,1)} async-done(((bf16[1024,768]{1,0:T(8,128)(2,1)}), bf16[2048,768]{1,0:T(8,128)(2,1)}) %all-gather.2.cloned.1.call-update) | async-done | bytes 3145744 | tf_op jit(solution)/shard_map/all_gather | solution.py:138
  488.5 13.0 %add_convert_fusion = bf16[768,2048]{1,0:T(8,128)(2,1)} fusion(f32[768,4096]{1,0:T(8,128)} %get-tuple-element.11, s32[]{:T(128)S(6)} %select_n.86, bf16[2048,768]{1,0:T(8,128)(2,1)} %all-gather.2.cloned.1.call-done, bf16[2048,2048]{1,0:T(8,128)(2,1)} %param.15), kind=kOutput, calls=%fused_computation.23 | convolution fusion | flops 6445596672 | bytes 20971524 | tf_op jit(solution)/shard_map/dot_general | solution.py:137
  (27 shorter events, 0.1 us)
Async XLA Ops:
  6.5 106.9 %all-to-all-start.1 = ((bf16[16,64,768]{2,1,0:T(8,128)(2,1)}), bf16[16,64,768]{2,1,0:T(8,128)(2,1)S(1)}, u32[]{:S(2)}, u32[]{:S(2)}) async-start(bf16[16,64,768]{2,1,0:T(8,128)(2,1)} %bitcast.149), calls=%async_computation.1 | async-start | bytes 3145728 | tf_op jit(solution)/shard_map/all_to_all | solution.py:125
  22.7 33.5 %copy-start.9 = (f32[4096]{0:T(1024)S(1)}, f32[4096]{0:T(1024)}, u32[]{:S(2)}) copy-start(f32[4096]{0:T(1024)} %param.10) | copy-start | bytes 49156
  84.1 11.0 %copy-start.8 = (f32[3,3,1024]{2,1,0:T(4,128)S(1)}, f32[3,3,1024]{2,1,0:T(4,128)}, u32[]{:S(2)}) copy-start(f32[3,3,1024]{2,1,0:T(4,128)} %param.12) | copy-start | bytes 110596
  92.5 3.8 collective-permute-start
  109.6 2.2 copy-start.3
  113.4 1.1 copy-start.7
  114.6 49.8 %all-to-all-start = ((bf16[16,64,768]{2,1,0:T(8,128)(2,1)}), bf16[16,64,768]{2,1,0:T(8,128)(2,1)S(1)}, u32[]{:S(2)}, u32[]{:S(2)}) async-start(bf16[16,64,768]{2,1,0:T(8,128)(2,1)} %bitcast.147), calls=%async_computation | async-start | bytes 3145728 | tf_op jit(solution)/shard_map/all_to_all | solution.py:124
  121.7 366.7 %all-gather.2.cloned.1.call-start = ((), (), s32[]{:S(2)}) async-start(), calls=%async_computation.3 | async-start | bytes 4718592 | tf_op jit(solution)/shard_map/all_gather | solution.py:138
  129.5 4.3 copy-start.4
  133.8 21.4 %copy-start = (f32[96,64,256]{2,0,1:T(8,128)}, f32[96,64,256]{2,0,1:T(8,128)S(1)}, u32[]{:S(2)}) copy-start(f32[96,64,256]{2,0,1:T(8,128)S(1)} %fusion.92) | copy-start | bytes 18874372
  136.6 18.6 %copy-start.1 = (f32[96,64,256]{2,0,1:T(8,128)}, f32[96,64,256]{2,0,1:T(8,128)S(1)}, u32[]{:S(2)}) copy-start(f32[96,64,256]{2,0,1:T(8,128)S(1)} %fusion.97) | copy-start | bytes 18874372
  170.3 4.4 copy-start.5
  196.2 18.4 %slice-start = ((s8[6291456]{0:T(1024)(128)(4,1)}), s8[4194304]{0:T(1024)(128)(4,1)S(1)}, s32[]{:S(2)}) async-start(s8[6291456]{0:T(1024)(128)(4,1)} %bitcast.134), calls=%async_computation.4 | async-start | bytes 8388608
  205.5 9.2 %slice-start.1 = ((s8[6291456]{0:T(1024)(128)(4,1)}), s8[2097152]{0:T(1024)(128)(4,1)S(1)}, s32[]{:S(2)}) async-start(s8[6291456]{0:T(1024)(128)(4,1)} %bitcast.134), calls=%async_computation.5 | async-start | bytes 4194304
  239.0 9.8 %copy-start.2 = (f32[64,96,256]{2,1,0:T(8,128)S(1)}, f32[64,96,256]{2,1,0:T(8,128)}, u32[]{:S(2)}) copy-start(f32[64,96,256]{2,1,0:T(8,128)} %get-tuple-element.6) | copy-start | bytes 18874372
  239.0 16.1 %slice-start.2 = ((s8[6291456]{0:T(1024)(128)(4,1)}), s8[4194304]{0:T(1024)(128)(4,1)S(1)}, s32[]{:S(2)}) async-start(s8[6291456]{0:T(1024)(128)(4,1)} %bitcast.136), calls=%async_computation.6 | async-start | bytes 8388608
  248.9 6.3 %slice-start.3 = ((s8[6291456]{0:T(1024)(128)(4,1)}), s8[2097152]{0:T(1024)(128)(4,1)S(1)}, s32[]{:S(2)}) async-start(s8[6291456]{0:T(1024)(128)(4,1)} %bitcast.136), calls=%async_computation.7 | async-start | bytes 4194304
  292.3 1.9 copy-start.6
Sparse Core Ops, SparseCore 0:
  443.1 45.3 all-gather.1
where the time goes:
time: 516 us; the launch traced here: 509 us
  matrix products  202 us (39%)
  local copies, waits for them, and re-layouts  101 us (20%)
  other arithmetic  85.9 us (17%)
  waiting for transfers between devices  45.5 us (9%)
  blocking collectives  42.1 us (8%)
  starting transfers between devices  17.7 us (3%)
  between operations  13.9 us (3%)
    dot_general x18, matrix products, contract(): jnp.einsum(form, left, right, precision=lax.Precision.HIGHEST, preferred_...  152 us
    unnamed x4, other arithmetic  67.5 us
    unnamed x33, local copies, waits for them, and re-layouts  50.2 us
    all_gather x1, waiting for transfers between devices, local(): lax.all_gather(gated, 'tp', axis=0, tiled=True)  45.5 us
    all_to_all x1, blocking collectives, local(): lax.all_to_all(outgoing.reshape(1, owned, -1), 'ctx', split_axis=2, conca...  42.1 us
    dot_general x1, matrix products, local(): jnp.dot(normed, w_in.reshape(width, 3 * chan_part), preferred_element_typ...  27.9 us
    dot_general x1, matrix products, local(): jnp.dot(lax.all_gather(gated, 'tp', axis=0, tiled=True).T, w_out, preferr...  13 us
    all_to_all x1, local copies, waits for them, and re-layouts, local(): lax.all_to_all(outgoing.reshape(1, owned, -1), 'ctx', split_axis=2, conca...  11.9 us
  transfers between devices with their start and end apart: 4, of which 1 were waited for; matrix products, arithmetic and copies ran while one was open for 27% of the time, Pallas kernels for 0%

commit v1 on v0

--- a/solution.py
+++ b/solution.py
@@ -128,8 +128,14 @@
     filter_full = arrived[1].reshape(owned, -1)
     convolved = causal_conv(product, filter_full)
     outgoing = (convolved + own_skip * product.astype(jnp.float32)).astype(jnp.bfloat16)
-    returned = lax.all_to_all(
-        outgoing.reshape(1, owned, -1), "ctx", split_axis=2, concat_axis=0, tiled=True
+    returned = jnp.concatenate(
+        lax.all_to_all(
+            jnp.stack(jnp.split(outgoing.reshape(1, owned, -1), lax.axis_size("ctx"), axis=2)),
+            "ctx",
+            0,
+            0,
+        ),
+        axis=0,
     )
     returned = returned.reshape(local_channels, positions)
     gated = (query_side.astype(jnp.float32) * returned.astype(jnp.float32)).astype(jnp.bfloat16)

time: 516 us -> 412 us (0.80)
  other arithmetic: 85.9 us -> 18.4 us
  local copies, waits for them, and re-layouts: 101 us -> 65.9 us
    unnamed x4 -> x3, other arithmetic: 67.5 us -> 0.33 us
    convert_element_type x3 -> x0, local copies, waits for them, and re-layouts: 12 us -> none  [the longest x1 9.96 us: local(): (convolved + own_skip * product.astype(jnp.float32)).astype(jnp.bfloat16)]
    all_to_all x1 -> x0, local copies, waits for them, and re-layouts: 11.9 us -> none  [local(): lax.all_to_all(outgoing.reshape(1, owned, -1), 'ctx', split_axis=2, conca...]
    unnamed x33 -> x44, local copies, waits for them, and re-layouts: 50.2 us -> 38.4 us
  transfers between devices with their start and end apart: 4 -> 4, of which waited for: 1 -> 1; matrix products, arithmetic and copies ran while one was open for 27% -> 34% of each run, Pallas kernels for 0% -> 0%
where the time goes in v1:
time: 412 us; the launch traced here: 405 us
  matrix products  202 us (49%)
  local copies, waits for them, and re-layouts  65.9 us (16%)
  waiting for transfers between devices  45.5 us (11%)
  blocking collectives  41.9 us (10%)
  other arithmetic  18.4 us (4%)
  starting transfers between devices  17.4 us (4%)
  between operations  14 us (3%)
    dot_general x18, matrix products, contract(): jnp.einsum(form, left, right, precision=lax.Precision.HIGHEST, preferred_...  152 us
    all_gather x1, waiting for transfers between devices, local(): lax.all_gather(gated, 'tp', axis=0, tiled=True)  45.5 us
    all_to_all x1, blocking collectives, local(): lax.all_to_all(jnp.stack(jnp.split(outgoing.reshape(1, owned, -1), lax.ax...  41.9 us
    unnamed x44, local copies, waits for them, and re-layouts  38.4 us
    dot_general x1, matrix products, local(): jnp.dot(normed, w_in.reshape(width, 3 * chan_part), preferred_element_typ...  27.9 us
    dot_general x1, matrix products, local(): jnp.dot(lax.all_gather(gated, 'tp', axis=0, tiled=True).T, w_out, preferr...  13 us
    dot_general x1, matrix products, local(): embedded = jnp.dot(one_hot, embed_table, preferred_element_type=jnp.float32)  8.78 us
  transfers between devices with their start and end apart: 4, of which 1 were waited for; matrix products, arithmetic and copies ran while one was open for 34% of the time, Pallas kernels for 0%

profile of v1, /device:TPU:0, one launch (start us, length us, event | category | flops | bytes accessed | tf_op | source)
XLA Modules:
  0.0 405.1 jit_solution(11385660098312642867)
XLA Ops:
  6.5 7.4 %all-to-all-start.1 = ((bf16[16,64,768]{2,1,0:T(8,128)(2,1)}), bf16[16,64,768]{2,1,0:T(8,128)(2,1)S(1)}, u32[]{:S(2)}, u32[]{:S(2)}) async-start(bf16[16,64,768]{2,1,0:T(8,128)(2,1)} %bitcast.199), calls=%async_computation.1 | async-start | bytes 3145728 | tf_op jit(solution)/shard_map/all_to_all | solution.py:125
  13.9 8.8 %multiply_reduce_fusion = (f32[768]{0:T(1024)S(1)}, f32[768,4096]{1,0:T(8,128)}) fusion(bf16[512,4096]{1,0:T(8,128)(2,1)} %param.9, s32[768]{0:T(1024)} %param.8), kind=kOutput, calls=%fused_computation.1 | convolution fusion | flops 3227909376 | bytes 16783360 | tf_op jit(solution)/shard_map/dot_general | solution.py:90
  22.7 33.6 %copy.36 = bf16[4096,3,1024]{0,2,1:T(8,128)(2,1)} copy(bf16[4096,3,1024]{2,0,1:T(8,128)(2,1)} %param.11) | data formatting | bytes 50331648 | tf_op args[3]
  56.3 0.0 copy-done.9
  56.3 27.9 %fusion.24 = bf16[768,3072]{1,0:T(8,128)(2,1)} fusion(bf16[4096,3072]{0,1:T(8,128)(2,1)} %bitcast.192, f32[768,4096]{1,0:T(8,128)} %get-tuple-element.11, f32[4096]{0:T(1024)S(1)} %copy-done.9, f32[768]{0:T(1024)S(1)} %add_rsqrt_fusion), kind=kOutput, calls=%fused_computation.39 | convolution fusion | flops 19339149312 | bytes 42486784 | tf_op jit(solution)/shard_map/dot_general | solution.py:95
  84.2 6.6 %copy.37 = bf16[768,3072]{0,1:T(8,128)(2,1)} copy(bf16[768,3072]{1,0:T(8,128)(2,1)} %fusion.24) | data formatting | bytes 9437184 | tf_op jit(solution)/shard_map/convert_element_type | solution.py:97
  90.9 1.4 slice.40
  92.3 0.3 copy.38
  92.6 2.5 collective-permute-start
  95.0 0.0 copy-done.8
  95.1 0.4 fusion.102
  95.5 0.8 dynamic_slice.7
  96.3 0.0 collective-permute-done
  96.3 0.4 copy.39
  96.7 4.8 %maximum_convert_fusion = f32[3,1024,770]{2,1,0:T(8,128)S(1)} fusion(bf16[3,1024,768]{2,1,0:T(8,128)(2,1)} %bitcast.194, bf16[3,1024,2]{2,1,0:T(8,128)(2,1)S(1)} %copy.39), kind=kLoop, calls=%fused_computation.38 | loop fusion | flops 9461760 | bytes 14192640 | tf_op jit(solution)/shard_map/convert_element_type | solution.py:102
  101.4 8.1 %fusion.1 = bf16[3,1024,768]{2,1,0:T(8,128)(2,1)S(1)} fusion(f32[3,1024,770]{2,1,0:T(8,128)S(1)} %maximum_convert_fusion, f32[3,1024]{1,0:T(4,128)S(1)} %get-tuple-element.8, f32[3,1024]{1,0:T(4,128)S(1)} %get-tuple-element.9, f32[3,1024]{1,0:T(4,128)S(1)} %get-tuple-element.7), kind=kLoop, calls=%fused_computation.4 | loop fusion | flops 14155776 | bytes 33067008 | tf_op jit(solution)/shard_map/convert_element_type | solution.py:107
  109.6 0.0 copy-start.3
  109.6 2.2 copy-done.3
  111.8 1.5 multiply_convert_fusion.4
  113.3 0.0 all-to-all-done.1
  113.3 1.1 copy-done.7
  114.5 7.3 %all-to-all-start = ((bf16[16,64,768]{2,1,0:T(8,128)(2,1)}), bf16[16,64,768]{2,1,0:T(8,128)(2,1)S(1)}, u32[]{:S(2)}, u32[]{:S(2)}) async-start(bf16[16,64,768]{2,1,0:T(8,128)(2,1)} %bitcast.198), calls=%async_computation | async-start | bytes 3145728 | tf_op jit(solution)/shard_map/all_to_all | solution.py:124
  121.8 0.3 all-gather.2.cloned.1.call-start
  122.1 3.4 copy.41
  125.5 3.7 reshape.130
  129.2 4.3 %fusion.108 = f32[96,64,256]{2,0,1:T(8,128)S(1)} fusion(bf16[64,48,256]{2,1,0:T(8,128)(2,1)} %reshape.130), kind=kOutput, calls=%fused_computation.134 | convolution fusion | flops 906011136 | bytes 7864320 | tf_op jit(solution)/shard_map/kn,cnm->ckm/dot_general | solution.py:27
  133.6 0.0 copy-done.4
  133.6 0.0 copy-start
  133.6 2.8 fusion.113
  136.4 0.0 copy-start.1
  136.4 9.2 %fusion.10 = f32[64,96,256]{2,1,0:T(8,128)} fusion(f32[96,64,256]{2,0,1:T(8,128)S(1)} %fusion.113, f32[96,64,256]{2,0,1:T(8,128)S(1)} %fusion.108, f32[96,256]{1,0:T(8,128)S(1)} %get-tuple-element.12, f32[96,256]{1,0:T(8,128)S(1)} %get-tuple-element.13), kind=kOutput, calls=%fused_computation.15 | convolution fusion | flops 4839047168 | bytes 19070976 | tf_op jit(solution)/shard_map/ckm,mj->ckj/dot_general | solution.py:27
  145.6 9.5 %fusion.6 = f32[64,96,256]{2,1,0:T(8,128)} fusion(f32[96,64,256]{2,0,1:T(8,128)S(1)} %fusion.113, f32[96,64,256]{2,0,1:T(8,128)S(1)} %fusion.108, f32[96,256]{1,0:T(8,128)S(1)} %get-tuple-element.12, f32[96,256]{1,0:T(8,128)S(1)} %get-tuple-element.13), kind=kOutput, calls=%fused_computation.11 | convolution fusion | flops 4839047168 | bytes 19070976 | tf_op jit(solution)/shard_map/ckm,mj->ckj/dot_general | solution.py:27
  155.1 0.0 copy-done
  155.1 0.0 copy-done.1
  155.1 9.2 %fusion.8 = f32[64,96,256]{2,1,0:T(8,128)} fusion(f32[96,64,256]{2,0,1:T(8,128)S(1)} %fusion.113, f32[96,64,256]{2,0,1:T(8,128)S(1)} %fusion.108, f32[96,256]{1,0:T(8,128)S(1)} %get-tuple-element.12, f32[96,256]{1,0:T(8,128)S(1)} %get-tuple-element.13), kind=kOutput, calls=%fused_computation.13 | convolution fusion | flops 4839047168 | bytes 19070976 | tf_op jit(solution)/shard_map/ckm,mj->ckj/dot_general | solution.py:27
  164.2 0.0 all-to-all-done
  164.2 2.0 copy.40
  166.3 4.2 %reshape.128 = bf16[64,48,256]{2,1,0:T(8,128)(2,1)} reshape(bf16[1,64,16,768]{3,2,1,0:T(8,128)(2,1)} %copy.40) | data formatting | bytes 3145728 | tf_op jit(solution)/shard_map/reshape | solution.py:74
  170.5 4.4 %fusion.110 = f32[64,256,96]{1,2,0:T(8,128)S(1)} fusion(bf16[64,48,256]{2,1,0:T(8,128)(2,1)} %reshape.128), kind=kOutput, calls=%fused_computation.136 | convolution fusion | flops 906011136 | bytes 7864320 | tf_op jit(solution)/shard_map/kn,cnm->ckm/dot_general | solution.py:27
  174.9 2.7 fusion.115
  177.6 9.2 %fusion.37 = f32[64,96,256]{2,1,0:T(8,128)} fusion(f32[64,256,96]{1,2,0:T(8,128)S(1)} %fusion.115, f32[64,256,96]{1,2,0:T(8,128)S(1)} %fusion.110, f32[96,256]{1,0:T(8,128)S(1)} %get-tuple-element.12, f32[96,256]{1,0:T(8,128)S(1)} %get-tuple-element.13), kind=kOutput, calls=%fused_computation.58 | convolution fusion | flops 4839047168 | bytes 19070976 | tf_op jit(solution)/shard_map/ckm,mj->ckj/dot_general | solution.py:27
  186.8 9.4 %fusion.41 = f32[64,96,256]{2,1,0:T(8,128)} fusion(f32[64,256,96]{1,2,0:T(8,128)S(1)} %fusion.115, f32[64,256,96]{1,2,0:T(8,128)S(1)} %fusion.110, f32[96,256]{1,0:T(8,128)S(1)} %get-tuple-element.12, f32[96,256]{1,0:T(8,128)S(1)} %get-tuple-element.13), kind=kOutput, calls=%fused_computation.60 | convolution fusion | flops 4839047168 | bytes 19070976 | tf_op jit(solution)/shard_map/ckm,mj->ckj/dot_general | solution.py:27
  196.2 9.2 %fusion.39 = f32[64,96,256]{2,1,0:T(8,128)} fusion(f32[64,256,96]{1,2,0:T(8,128)S(1)} %fusion.115, f32[64,256,96]{1,2,0:T(8,128)S(1)} %fusion.110, f32[96,256]{1,0:T(8,128)S(1)} %get-tuple-element.12, f32[96,256]{1,0:T(8,128)S(1)} %get-tuple-element.13), kind=kOutput, calls=%fused_computation.59 | convolution fusion | flops 4839047168 | bytes 19070976 | tf_op jit(solution)/shard_map/ckm,mj->ckj/dot_general | solution.py:27
  205.4 9.2 %fusion.35 = f32[64,96,256]{2,1,0:T(8,128)} fusion(f32[64,256,96]{1,2,0:T(8,128)S(1)} %fusion.115, f32[64,256,96]{1,2,0:T(8,128)S(1)} %fusion.110, f32[96,256]{1,0:T(8,128)S(1)} %get-tuple-element.12, f32[96,256]{1,0:T(8,128)S(1)} %get-tuple-element.13), kind=kOutput, calls=%fused_computation.57 | convolution fusion | flops 4839047168 | bytes 19070976 | tf_op jit(solution)/shard_map/ckm,mj->ckj/dot_general | solution.py:27
  214.6 0.0 slice-done
  214.6 24.3 %multiply_subtract_fusion = (f32[64,96,256]{2,1,0:T(8,128)}, f32[64,96,256]{2,1,0:T(8,128)}) fusion(f32[64,96,256]{2,1,0:T(8,128)} %fusion.8, f32[64,96,256]{2,1,0:T(8,128)} %fusion.35, f32[64,96,256]{2,1,0:T(8,128)} %fusion.39, f32[64,96,256]{2,1,0:T(8,128)} %fusion.10, f32[64,96,256]{2,1,0:T(8,128)} %fusion.6, f32[64,96,256]{2,1,0:T(8,128)} %fusion.41, ...), kind=kOutput, calls=%fused_computation.33 | convolution fusion | flops 4854775808 | bytes 69402624 | tf_op jit(solution)/shard_map/ckm,mj->ckj/dot_general | solution.py:27
  238.9 0.0 slice-start.2
  238.9 10.0 %fusion.51 = f32[64,96,256]{2,1,0:T(8,128)S(1)} fusion(f32[64,96,256]{2,1,0:T(8,128)} %get-tuple-element.6), kind=kOutput, calls=%fused_computation.70 | convolution fusion | flops 4832755712 | bytes 12582912 | tf_op jit(solution)/shard_map/ckj,mj->ckm/dot_general | solution.py:27
  249.0 0.0 slice-start.3
  249.0 6.3 %fusion.57 = f32[64,96,256]{2,1,0:T(8,128)S(1)} fusion(f32[64,96,256]{2,1,0:T(8,128)S(1)} %copy-done.2), kind=kOutput, calls=%fused_computation.76 | convolution fusion | flops 4832755712 | bytes 12582912 | tf_op jit(solution)/shard_map/ckj,mj->ckm/dot_general | solution.py:27
  255.3 6.4 %fusion.49 = f32[64,96,256]{2,1,0:T(8,128)S(1)} fusion(f32[64,96,256]{2,1,0:T(8,128)S(1)} %bitcast.191), kind=kOutput, calls=%fused_computation.68 | convolution fusion | flops 4832755712 | bytes 12582912 | tf_op jit(solution)/shard_map/ckj,mj->ckm/dot_general | solution.py:27
  261.7 8.9 %fusion.59 = f32[64,96,256]{2,1,0:T(8,128)} fusion(f32[64,96,256]{2,1,0:T(8,128)S(1)} %bitcast.191), kind=kOutput, calls=%fused_computation.78 | convolution fusion | flops 4832755712 | bytes 12582912 | tf_op jit(solution)/shard_map/ckj,mj->ckm/dot_general | solution.py:27
  270.7 8.3 %fusion.14 = f32[64,256,48]{1,2,0:T(8,128)} fusion(f32[96,256]{1,0:T(8,128)S(1)} %get-tuple-element.12, f32[96,256]{1,0:T(8,128)S(1)} %get-tuple-element.13, f32[64,96,256]{2,1,0:T(8,128)S(1)} %fusion.57, f32[64,96,256]{2,1,0:T(8,128)S(1)} %fusion.49, f32[64,96,256]{2,1,0:T(8,128)} %fusion.59, f32[64,96,256]{2,1,0:T(8,128)S(1)} %fusion.51), kind=kOutput, calls=%fused_computation.24 | convolution fusion | flops 913875456 | bytes 28508160 | tf_op jit(solution)/shard_map/kn,ckm->cnm/dot_general | solution.py:27
  279.0 8.9 %multiply_bitcast_fusion = f32[64,48,256]{2,1,0:T(8,128)} fusion(f32[64,256,48]{1,2,0:T(8,128)} %fusion.14, f32[96,256]{1,0:T(8,128)S(1)} %get-tuple-element.12, f32[96,256]{1,0:T(8,128)S(1)} %get-tuple-element.13, f32[64,96,256]{2,1,0:T(8,128)S(1)} %fusion.57, f32[64,96,256]{2,1,0:T(8,128)S(1)} %fusion.49, f32[64,96,256]{2,1,0:T(8,128)} %fusion.59, ...), kind=kOutput, calls=%fused_computation.44 | convolution fusion | flops 915448320 | bytes 31653888 | tf_op jit(solution)/shard_map/kn,ckm->cnm/dot_general | solution.py:27
  287.9 4.3 %reshape.131 = f32[1,64,12288]{2,1,0:T(8,128)} reshape(f32[64,48,256]{2,1,0:T(8,128)} %multiply_bitcast_fusion) | data formatting | bytes 6291456 | tf_op jit(solution)/shard_map/reshape | solution.py:82
  292.2 0.3 convert_bitcast_fusion
  292.5 0.3 copy.43
  292.8 1.2 copy-done.6
  294.1 0.3 add_convert_fusion.1
  294.7 41.9 %all_to_all.35 = bf16[16,1,64,768]{3,2,1,0:T(8,128)(2,1)S(1)} all-to-all(bf16[16,1,64,768]{3,2,1,0:T(8,128)(2,1)S(1)} %fusion.84), channel_id=1, replica_groups=mesh['ctx'=16,'tp'=2] {'ctx'}, dimensions={0} | all-to-all | bytes 3145728 | tf_op jit(solution)/shard_map/all_to_all | solution.py:132
  336.6 2.9 fusion.25
  339.6 0.0 all-gather.2.cloned.1.call-update
  339.6 45.5 %all-gather.2.cloned.1.call-done = bf16[2048,768]{1,0:T(8,128)(2,1)} async-done(((bf16[1024,768]{1,0:T(8,128)(2,1)}), bf16[2048,768]{1,0:T(8,128)(2,1)}) %all-gather.2.cloned.1.call-update) | async-done | bytes 3145744 | tf_op jit(solution)/shard_map/all_gather | solution.py:144
  385.1 13.0 %add_convert_fusion = bf16[768,2048]{1,0:T(8,128)(2,1)} fusion(f32[768,4096]{1,0:T(8,128)} %get-tuple-element.11, s32[]{:T(128)S(6)} %select_n.86, bf16[2048,768]{1,0:T(8,128)(2,1)} %all-gather.2.cloned.1.call-done, bf16[2048,2048]{1,0:T(8,128)(2,1)} %param.15), kind=kOutput, calls=%fused_computation.23 | convolution fusion | flops 6445596672 | bytes 20971524 | tf_op jit(solution)/shard_map/dot_general | solution.py:143
  (34 shorter events, 0.2 us)
Async XLA Ops:
  6.5 106.8 %all-to-all-start.1 = ((bf16[16,64,768]{2,1,0:T(8,128)(2,1)}), bf16[16,64,768]{2,1,0:T(8,128)(2,1)S(1)}, u32[]{:S(2)}, u32[]{:S(2)}) async-start(bf16[16,64,768]{2,1,0:T(8,128)(2,1)} %bitcast.199), calls=%async_computation.1 | async-start | bytes 3145728 | tf_op jit(solution)/shard_map/all_to_all | solution.py:125
  22.7 33.6 %copy-start.9 = (f32[4096]{0:T(1024)S(1)}, f32[4096]{0:T(1024)}, u32[]{:S(2)}) copy-start(f32[4096]{0:T(1024)} %param.10) | copy-start | bytes 49156
  84.2 10.8 %copy-start.8 = (f32[3,3,1024]{2,1,0:T(4,128)S(1)}, f32[3,3,1024]{2,1,0:T(4,128)}, u32[]{:S(2)}) copy-start(f32[3,3,1024]{2,1,0:T(4,128)} %param.12) | copy-start | bytes 110596
  92.6 3.7 collective-permute-start
  109.6 2.2 copy-start.3
  113.3 1.1 copy-start.7
  114.5 49.8 %all-to-all-start = ((bf16[16,64,768]{2,1,0:T(8,128)(2,1)}), bf16[16,64,768]{2,1,0:T(8,128)(2,1)S(1)}, u32[]{:S(2)}, u32[]{:S(2)}) async-start(bf16[16,64,768]{2,1,0:T(8,128)(2,1)} %bitcast.198), calls=%async_computation | async-start | bytes 3145728 | tf_op jit(solution)/shard_map/all_to_all | solution.py:124
  121.8 263.3 %all-gather.2.cloned.1.call-start = ((), (), s32[]{:S(2)}) async-start(), calls=%async_computation.3 | async-start | bytes 4718592 | tf_op jit(solution)/shard_map/all_gather | solution.py:144
  129.2 4.3 %copy-start.4 = (bf16[64,48,256]{2,1,0:T(8,128)(2,1)S(1)}, bf16[64,48,256]{2,1,0:T(8,128)(2,1)}, u32[]{:S(2)}) copy-start(bf16[64,48,256]{2,1,0:T(8,128)(2,1)} %reshape.130) | copy-start | bytes 4718596
  133.6 21.5 %copy-start = (f32[96,64,256]{2,0,1:T(8,128)}, f32[96,64,256]{2,0,1:T(8,128)S(1)}, u32[]{:S(2)}) copy-start(f32[96,64,256]{2,0,1:T(8,128)S(1)} %fusion.108) | copy-start | bytes 18874372
  136.4 18.7 %copy-start.1 = (f32[96,64,256]{2,0,1:T(8,128)}, f32[96,64,256]{2,0,1:T(8,128)S(1)}, u32[]{:S(2)}) copy-start(f32[96,64,256]{2,0,1:T(8,128)S(1)} %fusion.113) | copy-start | bytes 18874372
  170.4 4.4 %copy-start.5 = (bf16[64,48,256]{2,1,0:T(8,128)(2,1)S(1)}, bf16[64,48,256]{2,1,0:T(8,128)(2,1)}, u32[]{:S(2)}) copy-start(bf16[64,48,256]{2,1,0:T(8,128)(2,1)} %reshape.128) | copy-start | bytes 4718596
  196.2 18.4 %slice-start = ((s8[6291456]{0:T(1024)(128)(4,1)}), s8[4194304]{0:T(1024)(128)(4,1)S(1)}, s32[]{:S(2)}) async-start(s8[6291456]{0:T(1024)(128)(4,1)} %bitcast.188), calls=%async_computation.4 | async-start | bytes 8388608
  205.4 9.2 %slice-start.1 = ((s8[6291456]{0:T(1024)(128)(4,1)}), s8[2097152]{0:T(1024)(128)(4,1)S(1)}, s32[]{:S(2)}) async-start(s8[6291456]{0:T(1024)(128)(4,1)} %bitcast.188), calls=%async_computation.5 | async-start | bytes 4194304
  238.9 10.0 %copy-start.2 = (f32[64,96,256]{2,1,0:T(8,128)S(1)}, f32[64,96,256]{2,1,0:T(8,128)}, u32[]{:S(2)}) copy-start(f32[64,96,256]{2,1,0:T(8,128)} %get-tuple-element.6) | copy-start | bytes 18874372
  238.9 16.3 %slice-start.2 = ((s8[6291456]{0:T(1024)(128)(4,1)}), s8[4194304]{0:T(1024)(128)(4,1)S(1)}, s32[]{:S(2)}) async-start(s8[6291456]{0:T(1024)(128)(4,1)} %bitcast.190), calls=%async_computation.6 | async-start | bytes 8388608
  249.0 6.3 %slice-start.3 = ((s8[6291456]{0:T(1024)(128)(4,1)}), s8[2097152]{0:T(1024)(128)(4,1)S(1)}, s32[]{:S(2)}) async-start(s8[6291456]{0:T(1024)(128)(4,1)} %bitcast.190), calls=%async_computation.7 | async-start | bytes 4194304
  292.2 1.9 copy-start.6
Sparse Core Ops, SparseCore 0:
  339.7 45.3 all-gather.1
